TPU v7x, 32 devices: a whole 2x2x4 slice. The times are simulated.
32 devices in a mesh: group: 4 (over x, core), theta: 4 (over z), radial: 2 (over y).
Axes of the slice: x: 2, y: 2, z: 4, core: 2. Of those that a mesh axis runs over, the one named last changes fastest.
Arguments:
- scalars: float32 [26, 16, 16, 2048], P(None, 'group', 'radial', 'theta'), may hold values from 0.1 to 2
- axial_speed: float32 [16, 16, 2048], P('group', 'radial', 'theta'), may hold values from 0.2 to 0.9
- mixing: float32 [16, 16, 2048], P('group', 'radial', 'theta'), may hold values from 0.02 to 0.12
- reaction_rate: float32 [16, 16, 2048], P('group', 'radial', 'theta'), may hold values from 0.05 to 0.5
- reaction: float32 [20, 20], replicated, may hold values from -1.25 to 1.25
- nucleation: float32 [6], replicated, may hold values from 0.1 to 1
- coagulation: float32 [6], replicated, may hold values from 0.05 to 0.5
- inflow: float32 [26, 16, 2048], P(None, 'radial', 'theta'), may hold values from 0.1 to 2
- tile_weights: float32 [16, 128, 128], P('theta'), may hold values from -0.5 to 0.5
- donor_shift: int32 [16], P('theta'), may hold values from -1 to 1, as said below
- rotor_offset: int32 [1], replicated, may hold values from 0 to 2047
Outputs:
- advanced: float32 [26, 16, 16, 2048], P(None, 'group', 'radial', 'theta')
Inputs may be any that keep to these rules, and one draw needn't show every extreme that they name: `donor_shift`: in every aligned block of 4 tiles the first tile has offset -1 and the last offset 1.
All inputs are finite; a program needn't handle non-finite values.
Results may differ from a plain program's by a relative error of at most 0.00005.
Values sent between devices are 32-bit elements; how exact they have to be, the bound alone decides.
No kernel may reach another device: no remote copies, remote signals or barrier semaphores. Data moves between devices by JAX's collectives and lax.ppermute only.
A program may use at most 64 MiB of HBM per device.

v0:
```python
import jax
import jax.numpy as jnp
from jax import lax
from jax.sharding import PartitionSpec as P

SPECIES = 20
highest = lax.Precision.HIGHEST


def from_behind(block, axis, distance):
    devices = range(lax.axis_size(axis))
    route = [((i - distance) % len(devices), i) for i in devices]
    return lax.ppermute(block, axis, route)


def padded(array, sides, width, wrap):
    for axis, dim in sides:
        count, length = (lax.axis_size(axis), array.shape[dim])
        up = [(i, (i + 1) % count) for i in range(count if wrap else count - 1)]
        down = [(j, i) for i, j in up]
        last = lax.slice_in_dim(array, length - width, length, axis=dim)
        initial = lax.slice_in_dim(array, 0, width, axis=dim)
        before = lax.ppermute(last, axis, up)
        after = lax.ppermute(initial, axis, down)
        array = jnp.concatenate([before, array, after], axis=dim)
    return array


def from_behind_2(array, axis, by):
    count = lax.axis_size(axis)
    pairs = [(i, i + by) for i in range(count) if 0 <= i + by < count]
    return lax.ppermute(array, axis, pairs)


def rotate_rows(plane_rows, rotor_offset):
    sectors = lax.axis_size("theta")
    theta_cells = plane_rows.shape[1]
    device_hops = rotor_offset[0] // theta_cells
    cell_shift = rotor_offset[0] % theta_cells
    scattered = lax.all_to_all(plane_rows[None], "theta", split_axis=2, concat_axis=0, tiled=True)
    doubled = jnp.concatenate([scattered, scattered], axis=0)
    turned = lax.dynamic_slice_in_dim(doubled, sectors - device_hops, sectors, 0)
    shifted = lax.all_to_all(turned, "theta", split_axis=0, concat_axis=2, tiled=True)[0]
    previous = from_behind(shifted, "theta", 1)
    joined = jnp.concatenate([previous, shifted], axis=1)
    return lax.dynamic_slice_in_dim(joined, theta_cells - cell_shift, theta_cells, 1)


def apply_tiles(picked_rows, tile_weights):
    row_count, theta_cells = picked_rows.shape
    tile_blocks = picked_rows.reshape(row_count, theta_cells // 128, 128)
    result = jnp.einsum("rtk,tjk->rtj", tile_blocks, tile_weights, precision=highest)
    return result.reshape(row_count, theta_cells)


def couple_cells(plane_rows, tile_weights, donor_shift, rotor_offset):
    row_count, theta_cells = plane_rows.shape
    tile_count = theta_cells // 128
    rotated = rotate_rows(plane_rows, rotor_offset)
    extended = padded(rotated, (("theta", 1),), 128, True)
    tile_blocks = extended.reshape(row_count, tile_count + 2, 128)
    columns = lax.broadcasted_iota(jnp.int32, (tile_count, tile_count + 2), 1)
    targets = (
        lax.broadcasted_iota(jnp.int32, (tile_count, tile_count + 2), 0) + 1 + donor_shift[:, None]
    )
    chooser = (columns == targets).astype(jnp.float32)
    picked = jnp.einsum("rsk,ts->rtk", tile_blocks, chooser, precision=highest)
    return apply_tiles(picked.reshape(row_count, theta_cells), tile_weights)


def couple_rows(plane_rows, tile_weights, donor_shift, rotor_offset):
    return couple_cells(plane_rows, tile_weights, donor_shift, rotor_offset)


def local(
    scalars,
    axial_speed,
    mixing,
    reaction_rate,
    reaction,
    nucleation,
    coagulation,
    inflow,
    tile_weights,
    donor_shift,
    rotor_offset,
):
    variables, layers, radial_cells, theta_cells = scalars.shape
    groups = lax.axis_size("group")
    group_index = lax.axis_index("group")
    row_count = variables * radial_cells
    last_layer = scalars[:, layers - 1]
    received = from_behind_2(last_layer, "group", 1)
    coupled = couple_rows(
        received.reshape(row_count, theta_cells), tile_weights, donor_shift, rotor_offset
    )
    coupled = coupled.reshape(variables, radial_cells, theta_cells)
    ghost_plane = jnp.where(
        group_index == 0, inflow, jnp.where(group_index == groups - 1, coupled, received)
    )
    upstream = jnp.concatenate([ghost_plane[:, None], scalars[:, :-1]], axis=1)
    circle = padded(scalars, (("theta", 3),), 1, True)
    walls = padded(scalars, (("radial", 2),), 1, False)
    beside_all = circle[:, :, :, :-2] + circle[:, :, :, 2:]
    beside_all = beside_all + walls[:, :, 2:] + walls[:, :, :-2]
    laplace_term = beside_all - 4.0 * scalars
    species = scalars[:SPECIES]
    moments = scalars[SPECIES:]
    produced = jnp.dot(
        reaction,
        species.reshape(SPECIES, -1),
        precision=highest,
        preferred_element_type=jnp.float32,
    ).reshape(species.shape)
    growth = (
        nucleation[:, None, None, None] * species[SPECIES - 1]
        - coagulation[:, None, None, None] * moments[0] * moments
    )
    sources = jnp.concatenate([produced, growth], axis=0) * reaction_rate
    return scalars - axial_speed * (scalars - upstream) + mixing * laplace_term + sources


def solution(mesh):
    placed = (
        P(None, "group", "radial", "theta"),
        P("group", "radial", "theta"),
        P("group", "radial", "theta"),
        P("group", "radial", "theta"),
        P(),
        P(),
        P(),
        P(None, "radial", "theta"),
        P("theta", None, None),
        P("theta"),
        P(),
    )
    return jax.shard_map(
        local,
        mesh=mesh,
        in_specs=placed,
        out_specs=P(None, "group", "radial", "theta"),
        check_vma=False,
    )
```

profile of v0, /device:TPU:2, one launch (start us, length us, event | category | flops | bytes accessed | tf_op | source)
XLA Modules:
  0.0 98.0 jit_solution(16897832875728588099)
XLA Ops:
  0.0 2.5 %copy.82 = f32[26,4,8,512]{3,0,2,1:T(8,128)S(1)} copy(f32[26,4,8,512]{3,2,1,0:T(8,128)} %param.11) | data formatting | bytes 3407872 | tf_op args[0]
  2.6 1.9 %collective-permute-start = (f32[26,8,512]{2,0,1:T(8,128)S(1)}, f32[26,8,512]{2,0,1:T(8,128)S(1)}, u32[]{:S(2)}, u32[]{:S(2)}) collective-permute-start(f32[26,8,512]{2,0,1:T(8,128)S(1)} %slice_bitcast_fusion.2), channel_id=1, source_target_pairs={{0,8},{8,16},{16,24},{1,9},{9,17},{17,25},{2,10},{10,18},{18,26},{... | collective-permute-start | bytes 1277960 | tf_op jit(solution)/shard_map/ppermute | solution.py:32
  4.5 8.6 %collective-permute-done = f32[26,8,512]{2,0,1:T(8,128)S(1)} collective-permute-done((f32[26,8,512]{2,0,1:T(8,128)S(1)}, f32[26,8,512]{2,0,1:T(8,128)S(1)}, u32[]{:S(2)}, u32[]{:S(2)}) %collective-permute-start) | collective-permute-done | bytes 426016 | tf_op jit(solution)/shard_map/ppermute | solution.py:32
  13.1 0.8 copy-done.4
  14.1 1.0 %copy.73 = f32[1,208,512]{1,0,2:T(1,128)} copy(f32[1,208,512]{2,1,0:T(8,128)S(1)} %bitcast.63) | data formatting | bytes 851968 | tf_op jit(solution)/shard_map/broadcast_in_dim;reshape | solution.py:40
  15.1 4.9 %all-to-all-start = ((f32[1,208,512]{1,0,2:T(1,128)}), f32[1,208,512]{1,0,2:T(1,128)S(1)}, u32[]{:S(2)}, u32[]{:S(2)}) async-start(f32[1,208,512]{1,0,2:T(1,128)} %copy.73), calls=%async_computation | async-start | bytes 1048576 | tf_op jit(solution)/shard_map/all_to_all | solution.py:40
  20.0 0.8 fusion.21
  20.8 1.3 %collective-permute-start.6 = (f32[26,4,1,512]{3,0,2,1:T(8,128)}, f32[26,4,1,512]{3,0,2,1:T(8,128)}, u32[]{:S(2)}, u32[]{:S(2)}) collective-permute-start(f32[26,4,1,512]{3,0,2,1:T(8,128)} %get-tuple-element.7), channel_id=1, source_target_pairs={{1,0},{3,2},{5,4},{7,6},{9,8},{11,10},{13,12},{15,14},{17,16},{19,... | collective-permute-start | bytes 638984 | tf_op jit(solution)/shard_map/ppermute | solution.py:24
  22.2 6.1 %collective-permute-start.7 = (f32[26,4,1,512]{3,0,2,1:T(8,128)}, f32[26,4,1,512]{3,0,2,1:T(8,128)}, u32[]{:S(2)}, u32[]{:S(2)}) collective-permute-start(f32[26,4,1,512]{3,0,2,1:T(8,128)} %get-tuple-element.8), channel_id=1, source_target_pairs={{0,1},{2,3},{4,5},{6,7},{8,9},{10,11},{12,13},{14,15},{16,17},{18,... | collective-permute-start | bytes 638984 | tf_op jit(solution)/shard_map/ppermute | solution.py:23
  28.2 1.1 %fusion.20 = (f32[26,4,8,1]{3,0,2,1:T(8,128)}, f32[26,4,8,1]{3,0,2,1:T(8,128)}) fusion(f32[26,4,8,512]{3,0,2,1:T(8,128)S(1)} %copy.82), kind=kLoop, calls=%fused_computation.44 | loop fusion | bytes 13312 | tf_op jit(solution)/shard_map/slice | solution.py:21
  29.4 2.0 %collective-permute-start.4 = (f32[26,4,8,1]{3,0,2,1:T(8,128)}, f32[26,4,8,1]{3,0,2,1:T(8,128)}, u32[]{:S(2)}, u32[]{:S(2)}) collective-permute-start(f32[26,4,8,1]{3,0,2,1:T(8,128)} %get-tuple-element.5), channel_id=1, source_target_pairs={{0,2},{2,4},{4,6},{6,0},{1,3},{3,5},{5,7},{7,1},{8,10},{10,12},{12... | collective-permute-start | bytes 9992 | tf_op jit(solution)/shard_map/ppermute | solution.py:23
  32.1 8.1 %all-to-all-done = f32[1,208,512]{1,0,2:T(1,128)S(1)} async-done(((f32[1,208,512]{1,0,2:T(1,128)}), f32[1,208,512]{1,0,2:T(1,128)S(1)}, u32[]{:S(2)}, u32[]{:S(2)}) %all-to-all-start) | async-done | bytes 426016 | tf_op jit(solution)/shard_map/all_to_all | solution.py:40
  40.1 0.3 copy.74
  40.5 0.8 fusion.14
  41.3 3.5 %all-to-all-start.1 = ((f32[4,208,128]{2,1,0:T(8,128)}), f32[4,208,128]{2,1,0:T(8,128)S(1)}, u32[]{:S(2)}, u32[]{:S(2)}) async-start(f32[4,208,128]{2,1,0:T(8,128)} %fusion.14), calls=%async_computation.1 | async-start | bytes 851968 | tf_op jit(solution)/shard_map/all_to_all | solution.py:43
  44.8 0.9 slice_bitcast_fusion.4
  45.7 1.0 %fusion.11 = f32[6,4,8,512]{3,0,2,1:T(8,128)} fusion(f32[26,4,8,512]{3,0,2,1:T(8,128)S(1)} %copy.82, f32[4,8,512]{2,1,0:T(8,128)S(1)} %get-tuple-element.10, f32[6]{0:T(128)S(1)} %copy-done.9, f32[4,8,512]{2,1,0:T(8,128)S(1)} %get-tuple-element.9, f32[6]{0:T(128)S(1)} %copy-done.10), kind=kLoop, calls=%fused_computation.27 | loop fusion | flops 393216 | bytes 917552 | tf_op jit(solution)/shard_map/sub | solution.py:116
  46.7 2.5 %slice_bitcast_fusion.1 = f32[20,32,512]{2,1,0:T(8,128)} fusion(f32[26,4,8,512]{3,2,1,0:T(8,128)} %param.11), kind=kLoop, calls=%fused_computation.18 | loop fusion | bytes 2621440
  49.2 9.3 %all-to-all-done.1 = f32[4,208,128]{2,1,0:T(8,128)S(1)} async-done(((f32[4,208,128]{2,1,0:T(8,128)}), f32[4,208,128]{2,1,0:T(8,128)S(1)}, u32[]{:S(2)}, u32[]{:S(2)}) %all-to-all-start.1) | async-done | bytes 426016 | tf_op jit(solution)/shard_map/all_to_all | solution.py:43
  58.8 1.0 %copy-done.3 = f32[20,32,512]{2,1,0:T(8,128)S(1)} copy-done((f32[20,32,512]{2,1,0:T(8,128)S(1)}, f32[20,32,512]{2,1,0:T(8,128)}, u32[]{:S(2)}) %copy-start.3) | copy-done | bytes 1310744
  60.0 3.2 %fusion.9 = f32[20,4,8,512]{3,0,2,1:T(8,128)} fusion(f32[4,8,512,20]{2,1,0,3:T(8,128)S(1)} %slice_bitcast_fusion, f32[20,20]{1,0:T(8,128)S(1)} %copy-done.8), kind=kOutput, calls=%fused_computation.15 | convolution fusion | flops 78643200 | bytes 2623040 | tf_op jit(solution)/shard_map/dot_general | solution.py:109
  63.2 10.1 %collective-permute-done.1 = f32[208,512]{1,0:T(8,128)S(1)} collective-permute-done((f32[208,512]{1,0:T(8,128)S(1)}, f32[208,512]{1,0:T(8,128)S(1)}, u32[]{:S(2)}, u32[]{:S(2)}) %collective-permute-start.1) | collective-permute-done | bytes 426016 | tf_op jit(solution)/shard_map/ppermute | solution.py:13
  73.7 3.8 %collective-permute-start.3 = (f32[208,128]{1,0:T(8,128)S(1)}, f32[208,128]{1,0:T(8,128)S(1)}, u32[]{:S(2)}, u32[]{:S(2)}) collective-permute-start(f32[208,128]{1,0:T(8,128)S(1)} %get-tuple-element.12), channel_id=1, source_target_pairs={{2,0},{4,2},{6,4},{0,6},{3,1},{5,3},{7,5},{1,7},{10,8},{12,10},{14... | collective-permute-start | bytes 319496 | tf_op jit(solution)/shard_map/ppermute | solution.py:24
  77.5 2.7 %collective-permute-done.2 = f32[208,128]{1,0:T(8,128)S(1)} collective-permute-done((f32[208,128]{1,0:T(8,128)S(1)}, f32[208,128]{1,0:T(8,128)S(1)}, u32[]{:S(2)}, u32[]{:S(2)}) %collective-permute-start.2) | collective-permute-done | bytes 106528 | tf_op jit(solution)/shard_map/ppermute | solution.py:23
  80.3 0.6 convolution_bitcast_fusion.1
  80.9 0.6 convolution_bitcast_fusion
  81.5 0.9 copy.77
  82.5 1.9 %reshape_reshape.3 = f32[26,8,512]{2,1,0:T(8,128)} reshape(f32[208,4,128]{2,1,0:T(4,128)} %copy.77) | data formatting | bytes 851968 | tf_op jit(solution)/shard_map/reshape;reshape | solution.py:97
  84.4 1.9 %fusion.12 = f32[26,1,8,512]{3,0,2,1:T(8,128)S(1)} fusion(f32[26,8,512]{2,1,0:T(8,128)} %param.18, f32[26,8,512]{2,0,1:T(8,128)} %copy-done.4, f32[26,8,512]{2,1,0:T(8,128)} %reshape_reshape.3, pred[]{:T(512)S(6)} %eq.12, pred[]{:T(512)S(6)} %eq.11), kind=kLoop, calls=%fused_computation.30 | loop fusion | flops 212992 | bytes 1703938 | tf_op jit(solution)/shard_map/broadcast_in_dim | solution.py:101
  86.3 3.4 %collective-permute-done.5 = f32[26,4,8,1]{3,0,2,1:T(8,128)} collective-permute-done((f32[26,4,8,1]{3,0,2,1:T(8,128)}, f32[26,4,8,1]{3,0,2,1:T(8,128)}, u32[]{:S(2)}, u32[]{:S(2)}) %collective-permute-start.5) | collective-permute-done | bytes 3360 | tf_op jit(solution)/shard_map/ppermute | solution.py:24
  89.7 6.1 %fusion.4 = f32[26,4,8,512]{3,0,2,1:T(8,128)S(1)} fusion(f32[26,4,8,512]{3,0,2,1:T(8,128)} %copy-done.1, f32[26,4,1,512]{3,0,2,1:T(8,128)} %collective-permute-done.7, f32[26,4,1,512]{3,0,2,1:T(8,128)} %collective-permute-done.6, f32[26,4,8,1]{3,0,2,1:T(8,128)} %collective-permute-done.5, f32[26,4,8,1]{3,0,2,1:T(8,128)} %collective-permute-done.4, ...), kind=kLoop, calls=%fused_computation.5 | loop fusion | flops 7667712 | bytes 7444992 | tf_op jit(solution)/shard_map/add | solution.py:120
  95.8 2.2 %copy.94 = f32[26,4,8,512]{3,2,1,0:T(8,128)} copy(f32[26,4,8,512]{3,0,2,1:T(8,128)S(1)} %fusion.4) | data formatting | bytes 3407872 | tf_op jit(solution)/shard_map/add | solution.py:120
  (41 shorter events, 1.3 us)
Async XLA Ops:
  0.0 80.9 %copy-start = (f32[4,128,128]{2,1,0:T(8,128)S(1)}, f32[4,128,128]{2,1,0:T(8,128)}, u32[]{:S(2)}) copy-start(f32[4,128,128]{2,1,0:T(8,128)} %param.19) | copy-start | bytes 786436
  2.5 75.0 %copy-start.1 = (f32[26,4,8,512]{3,0,2,1:T(8,128)}, f32[26,4,8,512]{3,0,2,1:T(8,128)S(1)}, u32[]{:S(2)}) copy-start(f32[26,4,8,512]{3,0,2,1:T(8,128)S(1)} %copy.82) | copy-start | bytes 5111812
  2.6 10.5 %collective-permute-start = (f32[26,8,512]{2,0,1:T(8,128)S(1)}, f32[26,8,512]{2,0,1:T(8,128)S(1)}, u32[]{:S(2)}, u32[]{:S(2)}) collective-permute-start(f32[26,8,512]{2,0,1:T(8,128)S(1)} %slice_bitcast_fusion.2), channel_id=1, source_target_pairs={{0,8},{8,16},{16,24},{1,9},{9,17},{17,25},{2,10},{10,18},{18,26},{... | collective-permute-start | bytes 1277960 | tf_op jit(solution)/shard_map/ppermute | solution.py:32
  13.1 0.8 copy-start.4
  15.1 25.0 %all-to-all-start = ((f32[1,208,512]{1,0,2:T(1,128)}), f32[1,208,512]{1,0,2:T(1,128)S(1)}, u32[]{:S(2)}, u32[]{:S(2)}) async-start(f32[1,208,512]{1,0,2:T(1,128)} %copy.73), calls=%async_computation | async-start | bytes 1048576 | tf_op jit(solution)/shard_map/all_to_all | solution.py:40
  20.8 68.8 %collective-permute-start.6 = (f32[26,4,1,512]{3,0,2,1:T(8,128)}, f32[26,4,1,512]{3,0,2,1:T(8,128)}, u32[]{:S(2)}, u32[]{:S(2)}) collective-permute-start(f32[26,4,1,512]{3,0,2,1:T(8,128)} %get-tuple-element.7), channel_id=1, source_target_pairs={{1,0},{3,2},{5,4},{7,6},{9,8},{11,10},{13,12},{15,14},{17,16},{19,... | collective-permute-start | bytes 638984 | tf_op jit(solution)/shard_map/ppermute | solution.py:24
  22.1 23.5 %copy-start.9 = (f32[6]{0:T(128)S(1)}, f32[6]{0:T(128)}, u32[]{:S(2)}) copy-start(f32[6]{0:T(128)} %param.17) | copy-start | bytes 76
  22.1 23.5 %copy-start.10 = (f32[6]{0:T(128)S(1)}, f32[6]{0:T(128)}, u32[]{:S(2)}) copy-start(f32[6]{0:T(128)} %param.16) | copy-start | bytes 76
  22.2 67.5 %collective-permute-start.7 = (f32[26,4,1,512]{3,0,2,1:T(8,128)}, f32[26,4,1,512]{3,0,2,1:T(8,128)}, u32[]{:S(2)}, u32[]{:S(2)}) collective-permute-start(f32[26,4,1,512]{3,0,2,1:T(8,128)} %get-tuple-element.8), channel_id=1, source_target_pairs={{0,1},{2,3},{4,5},{6,7},{8,9},{10,11},{12,13},{14,15},{16,17},{18,... | collective-permute-start | bytes 638984 | tf_op jit(solution)/shard_map/ppermute | solution.py:23
  29.4 56.9 %collective-permute-start.4 = (f32[26,4,8,1]{3,0,2,1:T(8,128)}, f32[26,4,8,1]{3,0,2,1:T(8,128)}, u32[]{:S(2)}, u32[]{:S(2)}) collective-permute-start(f32[26,4,8,1]{3,0,2,1:T(8,128)} %get-tuple-element.5), channel_id=1, source_target_pairs={{0,2},{2,4},{4,6},{6,0},{1,3},{3,5},{5,7},{7,1},{8,10},{10,12},{12... | collective-permute-start | bytes 9992 | tf_op jit(solution)/shard_map/ppermute | solution.py:23
  41.3 17.2 %all-to-all-start.1 = ((f32[4,208,128]{2,1,0:T(8,128)}), f32[4,208,128]{2,1,0:T(8,128)S(1)}, u32[]{:S(2)}, u32[]{:S(2)}) async-start(f32[4,208,128]{2,1,0:T(8,128)} %fusion.14), calls=%async_computation.1 | async-start | bytes 851968 | tf_op jit(solution)/shard_map/all_to_all | solution.py:43
  58.5 1.3 %copy-start.3 = (f32[20,32,512]{2,1,0:T(8,128)S(1)}, f32[20,32,512]{2,1,0:T(8,128)}, u32[]{:S(2)}) copy-start(f32[20,32,512]{2,1,0:T(8,128)} %slice_bitcast_fusion.1) | copy-start | bytes 3932164
  58.5 1.5 %copy-start.8 = (f32[20,20]{1,0:T(8,128)S(1)}, f32[20,20]{1,0:T(8,128)}, u32[]{:S(2)}) copy-start(f32[20,20]{1,0:T(8,128)} %param.15) | copy-start | bytes 4804
  58.7 14.5 %collective-permute-start.1 = (f32[208,512]{1,0:T(8,128)S(1)}, f32[208,512]{1,0:T(8,128)S(1)}, u32[]{:S(2)}, u32[]{:S(2)}) collective-permute-start(f32[208,512]{1,0:T(8,128)S(1)} %bitcast.60), channel_id=1, source_target_pairs={{6,0},{0,2},{2,4},{4,6},{7,1},{1,3},{3,5},{5,7},{14,8},{8,10},{10,... | collective-permute-start | bytes 1277960 | tf_op jit(solution)/shard_map/ppermute | solution.py:13
  60.0 17.5 %copy-start.11 = (s32[4]{0:T(128)S(1)}, s32[4]{0:T(128)}, u32[]{:S(2)}) copy-start(s32[4]{0:T(128)} %param.20) | copy-start | bytes 52
  73.6 6.6 %collective-permute-start.2 = (f32[208,128]{1,0:T(8,128)S(1)}, f32[208,128]{1,0:T(8,128)S(1)}, u32[]{:S(2)}, u32[]{:S(2)}) collective-permute-start(f32[208,128]{1,0:T(8,128)S(1)} %get-tuple-element.11), channel_id=1, source_target_pairs={{0,2},{2,4},{4,6},{6,0},{1,3},{3,5},{5,7},{7,1},{8,10},{10,12},{12... | collective-permute-start | bytes 319496 | tf_op jit(solution)/shard_map/ppermute | solution.py:23
  73.7 6.5 %collective-permute-start.3 = (f32[208,128]{1,0:T(8,128)S(1)}, f32[208,128]{1,0:T(8,128)S(1)}, u32[]{:S(2)}, u32[]{:S(2)}) collective-permute-start(f32[208,128]{1,0:T(8,128)S(1)} %get-tuple-element.12), channel_id=1, source_target_pairs={{2,0},{4,2},{6,4},{0,6},{3,1},{5,3},{7,5},{1,7},{10,8},{12,10},{14... | collective-permute-start | bytes 319496 | tf_op jit(solution)/shard_map/ppermute | solution.py:24
  80.2 9.5 %collective-permute-start.5 = (f32[26,4,8,1]{3,0,2,1:T(8,128)}, f32[26,4,8,1]{3,0,2,1:T(8,128)}, u32[]{:S(2)}, u32[]{:S(2)}) collective-permute-start(f32[26,4,8,1]{3,0,2,1:T(8,128)} %get-tuple-element.6), channel_id=1, source_target_pairs={{2,0},{4,2},{6,4},{0,6},{3,1},{5,3},{7,5},{1,7},{10,8},{12,10},{14... | collective-permute-start | bytes 9992 | tf_op jit(solution)/shard_map/ppermute | solution.py:24
  80.9 8.8 %slice-start = ((f32[26,4,8,512]{3,0,2,1:T(8,128)}), f32[26,3,8,512]{3,0,2,1:T(8,128)S(1)}, s32[]{:S(2)}) async-start(f32[26,4,8,512]{3,0,2,1:T(8,128)} %copy-done.1), calls=%async_computation.2 | async-start | bytes 3145728 | tf_op jit(solution)/shard_map/slice | solution.py:101
  80.9 8.8 %copy-start.2 = (f32[20,4,8,512]{3,0,2,1:T(8,128)S(1)}, f32[20,4,8,512]{3,0,2,1:T(8,128)}, u32[]{:S(2)}) copy-start(f32[20,4,8,512]{3,0,2,1:T(8,128)} %fusion.9) | copy-start | bytes 3932164
  80.9 8.8 %copy-start.6 = (f32[4,8,512]{2,1,0:T(8,128)S(1)}, f32[4,8,512]{2,1,0:T(8,128)}, u32[]{:S(2)}) copy-start(f32[4,8,512]{2,1,0:T(8,128)} %param.14) | copy-start | bytes 196612
  80.9 8.8 %copy-start.7 = (f32[4,8,512]{2,1,0:T(8,128)S(1)}, f32[4,8,512]{2,1,0:T(8,128)}, u32[]{:S(2)}) copy-start(f32[4,8,512]{2,1,0:T(8,128)} %param.13) | copy-start | bytes 196612
  84.4 5.3 %copy-start.5 = (f32[6,4,8,512]{3,0,2,1:T(8,128)S(1)}, f32[6,4,8,512]{3,0,2,1:T(8,128)}, u32[]{:S(2)}) copy-start(f32[6,4,8,512]{3,0,2,1:T(8,128)} %fusion.11) | copy-start | bytes 1179652
where the time goes:
time: 98.5 us; the launch traced here: 98 us
  waiting for transfers between devices  42.1 us (43%)
  starting transfers between devices  23.6 us (24%)
  local copies, waits for them, and re-layouts  16.9 us (17%)
  other arithmetic  10.1 us (10%)
  matrix products  4.31 us (4%)
  between operations  0.99 us (1%)
    ppermute x1, waiting for transfers between devices, from_behind(): return lax.ppermute(block, axis, route)  10.1 us
    all_to_all x1, waiting for transfers between devices, rotate_rows(): lax.all_to_all(turned, 'theta', split_axis=0, concat_axis=2, tiled=True)[0]  9.34 us
    ppermute x1, waiting for transfers between devices, from_behind_2(): return lax.ppermute(array, axis, pairs)  8.57 us
    ppermute x3, starting transfers between devices, padded(): before = lax.ppermute(last, axis, up)  8.16 us
    all_to_all x1, waiting for transfers between devices, rotate_rows(): lax.all_to_all(plane_rows[None], 'theta', split_axis=2, concat_axis=0, ti...  8.06 us
    unnamed x27, local copies, waits for them, and re-layouts  6.92 us
    add x1, other arithmetic, local(): scalars - axial_speed * (scalars - upstream) + mixing * laplace_term  6.1 us
    ppermute x3, starting transfers between devices, padded(): after = lax.ppermute(initial, axis, down)  5.09 us
  transfers between devices with their start and end apart: 10, of which 6 were waited for; matrix products, arithmetic and copies ran while one was open for 18% of the time, Pallas kernels for 0%

commit v1 on v0

--- a/solution.py
+++ b/solution.py
@@ -40,7 +40,10 @@
     scattered = lax.all_to_all(plane_rows[None], "theta", split_axis=2, concat_axis=0, tiled=True)
     doubled = jnp.concatenate([scattered, scattered], axis=0)
     turned = lax.dynamic_slice_in_dim(doubled, sectors - device_hops, sectors, 0)
-    shifted = lax.all_to_all(turned, "theta", split_axis=0, concat_axis=2, tiled=True)[0]
+    shifted = jnp.concatenate(
+        lax.all_to_all(jnp.stack(jnp.split(turned, lax.axis_size("theta"), axis=0)), "theta", 0, 0),
+        axis=2,
+    )[0]
     previous = from_behind(shifted, "theta", 1)
     joined = jnp.concatenate([previous, shifted], axis=1)
     return lax.dynamic_slice_in_dim(joined, theta_cells - cell_shift, theta_cells, 1)

time: 98.5 us -> 98.8 us (level)
  no operation moved by 1% of the time
where the time goes in v1:
time: 98.8 us; the launch traced here: 98.3 us
  waiting for transfers between devices  42.3 us (43%)
  starting transfers between devices  23.5 us (24%)
  local copies, waits for them, and re-layouts  17 us (17%)
  other arithmetic  10.3 us (10%)
  matrix products  4.31 us (4%)
  between operations  0.99 us (1%)
    ppermute x1, waiting for transfers between devices, from_behind(): return lax.ppermute(block, axis, route)  10.1 us
    all_to_all x1, waiting for transfers between devices, rotate_rows(): lax.all_to_all(jnp.stack(jnp.split(turned, lax.axis_size('theta'), axis=0...  9.32 us
    ppermute x1, waiting for transfers between devices, from_behind_2(): return lax.ppermute(array, axis, pairs)  8.57 us
    all_to_all x1, waiting for transfers between devices, rotate_rows(): lax.all_to_all(plane_rows[None], 'theta', split_axis=2, concat_axis=0, ti...  8.27 us
    ppermute x3, starting transfers between devices, padded(): before = lax.ppermute(last, axis, up)  8.05 us
    unnamed x27, local copies, waits for them, and re-layouts  6.91 us
    add x1, other arithmetic, local(): scalars - axial_speed * (scalars - upstream) + mixing * laplace_term  6.18 us
    ppermute x3, starting transfers between devices, padded(): after = lax.ppermute(initial, axis, down)  5.09 us
  transfers between devices with their start and end apart: 10, of which 6 were waited for; matrix products, arithmetic and copies ran while one was open for 18% of the time, Pallas kernels for 0%

profile of v1, /device:TPU:2, one launch (start us, length us, event | category | flops | bytes accessed | tf_op | source)
XLA Modules:
  0.0 98.3 jit_solution(1481095927739889467)
XLA Ops:
  0.0 2.5 %copy.66 = f32[26,4,8,512]{3,0,2,1:T(8,128)S(1)} copy(f32[26,4,8,512]{3,2,1,0:T(8,128)} %param.11) | data formatting | bytes 3407872 | tf_op args[0]
  2.6 1.9 %collective-permute-start = (f32[26,8,512]{2,0,1:T(8,128)S(1)}, f32[26,8,512]{2,0,1:T(8,128)S(1)}, u32[]{:S(2)}, u32[]{:S(2)}) collective-permute-start(f32[26,8,512]{2,0,1:T(8,128)S(1)} %slice_bitcast_fusion.2), channel_id=1, source_target_pairs={{0,8},{8,16},{16,24},{1,9},{9,17},{17,25},{2,10},{10,18},{18,26},{... | collective-permute-start | bytes 1277960 | tf_op jit(solution)/shard_map/ppermute | solution.py:32
  4.5 8.6 %collective-permute-done = f32[26,8,512]{2,0,1:T(8,128)S(1)} collective-permute-done((f32[26,8,512]{2,0,1:T(8,128)S(1)}, f32[26,8,512]{2,0,1:T(8,128)S(1)}, u32[]{:S(2)}, u32[]{:S(2)}) %collective-permute-start) | collective-permute-done | bytes 426016 | tf_op jit(solution)/shard_map/ppermute | solution.py:32
  13.1 0.8 copy-done.4
  14.1 1.0 %copy.57 = f32[1,208,512]{1,0,2:T(1,128)} copy(f32[1,208,512]{2,1,0:T(8,128)S(1)} %bitcast.69) | data formatting | bytes 851968 | tf_op jit(solution)/shard_map/broadcast_in_dim;reshape | solution.py:40
  15.1 4.9 %all-to-all-start = ((f32[1,208,512]{1,0,2:T(1,128)}), f32[1,208,512]{1,0,2:T(1,128)S(1)}, u32[]{:S(2)}, u32[]{:S(2)}) async-start(f32[1,208,512]{1,0,2:T(1,128)} %copy.57), calls=%async_computation | async-start | bytes 1048576 | tf_op jit(solution)/shard_map/all_to_all | solution.py:40
  20.0 0.8 fusion.21
  20.9 1.3 %collective-permute-start.6 = (f32[26,4,1,512]{3,0,2,1:T(8,128)}, f32[26,4,1,512]{3,0,2,1:T(8,128)}, u32[]{:S(2)}, u32[]{:S(2)}) collective-permute-start(f32[26,4,1,512]{3,0,2,1:T(8,128)} %get-tuple-element.7), channel_id=1, source_target_pairs={{1,0},{3,2},{5,4},{7,6},{9,8},{11,10},{13,12},{15,14},{17,16},{19,... | collective-permute-start | bytes 638984 | tf_op jit(solution)/shard_map/ppermute | solution.py:24
  22.1 6.0 %collective-permute-start.7 = (f32[26,4,1,512]{3,0,2,1:T(8,128)}, f32[26,4,1,512]{3,0,2,1:T(8,128)}, u32[]{:S(2)}, u32[]{:S(2)}) collective-permute-start(f32[26,4,1,512]{3,0,2,1:T(8,128)} %get-tuple-element.8), channel_id=1, source_target_pairs={{0,1},{2,3},{4,5},{6,7},{8,9},{10,11},{12,13},{14,15},{16,17},{18,... | collective-permute-start | bytes 638984 | tf_op jit(solution)/shard_map/ppermute | solution.py:23
  28.1 1.2 %fusion.20 = (f32[26,4,8,1]{3,0,2,1:T(8,128)}, f32[26,4,8,1]{3,0,2,1:T(8,128)}) fusion(f32[26,4,8,512]{3,0,2,1:T(8,128)S(1)} %copy.66), kind=kLoop, calls=%fused_computation.49 | loop fusion | bytes 13312 | tf_op jit(solution)/shard_map/slice | solution.py:21
  29.3 2.0 %collective-permute-start.4 = (f32[26,4,8,1]{3,0,2,1:T(8,128)}, f32[26,4,8,1]{3,0,2,1:T(8,128)}, u32[]{:S(2)}, u32[]{:S(2)}) collective-permute-start(f32[26,4,8,1]{3,0,2,1:T(8,128)} %get-tuple-element.5), channel_id=1, source_target_pairs={{0,2},{2,4},{4,6},{6,0},{1,3},{3,5},{5,7},{7,1},{8,10},{10,12},{12... | collective-permute-start | bytes 9992 | tf_op jit(solution)/shard_map/ppermute | solution.py:23
  32.0 8.3 %all-to-all-done = f32[1,208,512]{1,0,2:T(1,128)S(1)} async-done(((f32[1,208,512]{1,0,2:T(1,128)}), f32[1,208,512]{1,0,2:T(1,128)S(1)}, u32[]{:S(2)}, u32[]{:S(2)}) %all-to-all-start) | async-done | bytes 426016 | tf_op jit(solution)/shard_map/all_to_all | solution.py:40
  40.3 0.3 copy.58
  40.7 0.8 pad_maximum_fusion.5
  41.5 3.5 %all-to-all-start.1 = ((f32[4,1,208,128]{3,2,1,0:T(8,128)}), f32[4,1,208,128]{3,2,1,0:T(8,128)S(1)}, u32[]{:S(2)}, u32[]{:S(2)}) async-start(f32[4,1,208,128]{3,2,1,0:T(8,128)} %pad_maximum_fusion.5), calls=%async_computation.1 | async-start | bytes 851968 | tf_op jit(solution)/shard_map/all_to_all | solution.py:44
  45.0 0.9 slice_bitcast_fusion.8
  45.9 1.0 %fusion.11 = f32[6,4,8,512]{3,0,2,1:T(8,128)} fusion(f32[26,4,8,512]{3,0,2,1:T(8,128)S(1)} %copy.66, f32[4,8,512]{2,1,0:T(8,128)S(1)} %get-tuple-element.10, f32[6]{0:T(128)S(1)} %copy-done.9, f32[4,8,512]{2,1,0:T(8,128)S(1)} %get-tuple-element.9, f32[6]{0:T(128)S(1)} %copy-done.10), kind=kLoop, calls=%fused_computation.27 | loop fusion | flops 393216 | bytes 917552 | tf_op jit(solution)/shard_map/sub | solution.py:119
  46.9 2.5 %slice_bitcast_fusion.1 = f32[20,32,512]{2,1,0:T(8,128)} fusion(f32[26,4,8,512]{3,2,1,0:T(8,128)} %param.11), kind=kLoop, calls=%fused_computation.18 | loop fusion | bytes 2621440
  49.4 9.3 %all-to-all-done.1 = f32[4,1,208,128]{3,2,1,0:T(8,128)S(1)} async-done(((f32[4,1,208,128]{3,2,1,0:T(8,128)}), f32[4,1,208,128]{3,2,1,0:T(8,128)S(1)}, u32[]{:S(2)}, u32[]{:S(2)}) %all-to-all-start.1) | async-done | bytes 426016 | tf_op jit(solution)/shard_map/all_to_all | solution.py:44
  59.0 1.0 %copy-done.3 = f32[20,32,512]{2,1,0:T(8,128)S(1)} copy-done((f32[20,32,512]{2,1,0:T(8,128)S(1)}, f32[20,32,512]{2,1,0:T(8,128)}, u32[]{:S(2)}) %copy-start.3) | copy-done | bytes 1310744
  60.2 3.2 %fusion.9 = f32[20,4,8,512]{3,0,2,1:T(8,128)} fusion(f32[4,8,512,20]{2,1,0,3:T(8,128)S(1)} %slice_bitcast_fusion, f32[20,20]{1,0:T(8,128)S(1)} %copy-done.8), kind=kOutput, calls=%fused_computation.15 | convolution fusion | flops 78643200 | bytes 2623040 | tf_op jit(solution)/shard_map/dot_general | solution.py:112
  63.4 10.1 %collective-permute-done.1 = f32[208,512]{1,0:T(8,128)S(1)} collective-permute-done((f32[208,512]{1,0:T(8,128)S(1)}, f32[208,512]{1,0:T(8,128)S(1)}, u32[]{:S(2)}, u32[]{:S(2)}) %collective-permute-start.1) | collective-permute-done | bytes 426016 | tf_op jit(solution)/shard_map/ppermute | solution.py:13
  73.9 3.8 %collective-permute-start.3 = (f32[208,128]{1,0:T(8,128)S(1)}, f32[208,128]{1,0:T(8,128)S(1)}, u32[]{:S(2)}, u32[]{:S(2)}) collective-permute-start(f32[208,128]{1,0:T(8,128)S(1)} %get-tuple-element.12), channel_id=1, source_target_pairs={{2,0},{4,2},{6,4},{0,6},{3,1},{5,3},{7,5},{1,7},{10,8},{12,10},{14... | collective-permute-start | bytes 319496 | tf_op jit(solution)/shard_map/ppermute | solution.py:24
  77.7 2.7 %collective-permute-done.2 = f32[208,128]{1,0:T(8,128)S(1)} collective-permute-done((f32[208,128]{1,0:T(8,128)S(1)}, f32[208,128]{1,0:T(8,128)S(1)}, u32[]{:S(2)}, u32[]{:S(2)}) %collective-permute-start.2) | collective-permute-done | bytes 106528 | tf_op jit(solution)/shard_map/ppermute | solution.py:23
  80.5 0.6 convolution_bitcast_fusion.1
  81.2 0.6 convolution_bitcast_fusion
  81.7 0.9 copy.61
  82.7 1.9 %reshape_reshape.3 = f32[26,8,512]{2,1,0:T(8,128)} reshape(f32[208,4,128]{2,1,0:T(4,128)} %copy.61) | data formatting | bytes 851968 | tf_op jit(solution)/shard_map/reshape;reshape | solution.py:100
  84.6 1.9 %fusion.12 = f32[26,1,8,512]{3,0,2,1:T(8,128)S(1)} fusion(f32[26,8,512]{2,1,0:T(8,128)} %param.18, f32[26,8,512]{2,0,1:T(8,128)} %copy-done.4, f32[26,8,512]{2,1,0:T(8,128)} %reshape_reshape.3, pred[]{:T(512)S(6)} %eq.12, pred[]{:T(512)S(6)} %eq.11), kind=kLoop, calls=%fused_computation.30 | loop fusion | flops 212992 | bytes 1703938 | tf_op jit(solution)/shard_map/broadcast_in_dim | solution.py:104
  86.5 3.3 %collective-permute-done.5 = f32[26,4,8,1]{3,0,2,1:T(8,128)} collective-permute-done((f32[26,4,8,1]{3,0,2,1:T(8,128)}, f32[26,4,8,1]{3,0,2,1:T(8,128)}, u32[]{:S(2)}, u32[]{:S(2)}) %collective-permute-start.5) | collective-permute-done | bytes 3360 | tf_op jit(solution)/shard_map/ppermute | solution.py:24
  89.9 6.2 %fusion.4 = f32[26,4,8,512]{3,0,2,1:T(8,128)S(1)} fusion(f32[26,4,8,512]{3,0,2,1:T(8,128)} %copy-done.1, f32[26,4,1,512]{3,0,2,1:T(8,128)} %collective-permute-done.7, f32[26,4,1,512]{3,0,2,1:T(8,128)} %collective-permute-done.6, f32[26,4,8,1]{3,0,2,1:T(8,128)} %collective-permute-done.5, f32[26,4,8,1]{3,0,2,1:T(8,128)} %collective-permute-done.4, ...), kind=kLoop, calls=%fused_computation.5 | loop fusion | flops 7667712 | bytes 7444992 | tf_op jit(solution)/shard_map/add | solution.py:123
  96.1 2.2 %copy.78 = f32[26,4,8,512]{3,2,1,0:T(8,128)} copy(f32[26,4,8,512]{3,0,2,1:T(8,128)S(1)} %fusion.4) | data formatting | bytes 3407872 | tf_op jit(solution)/shard_map/add | solution.py:123
  (43 shorter events, 1.4 us)
Async XLA Ops:
  0.0 81.1 %copy-start = (f32[4,128,128]{2,1,0:T(8,128)S(1)}, f32[4,128,128]{2,1,0:T(8,128)}, u32[]{:S(2)}) copy-start(f32[4,128,128]{2,1,0:T(8,128)} %param.19) | copy-start | bytes 786436
  2.5 75.2 %copy-start.1 = (f32[26,4,8,512]{3,0,2,1:T(8,128)}, f32[26,4,8,512]{3,0,2,1:T(8,128)S(1)}, u32[]{:S(2)}) copy-start(f32[26,4,8,512]{3,0,2,1:T(8,128)S(1)} %copy.66) | copy-start | bytes 5111812
  2.6 10.5 %collective-permute-start = (f32[26,8,512]{2,0,1:T(8,128)S(1)}, f32[26,8,512]{2,0,1:T(8,128)S(1)}, u32[]{:S(2)}, u32[]{:S(2)}) collective-permute-start(f32[26,8,512]{2,0,1:T(8,128)S(1)} %slice_bitcast_fusion.2), channel_id=1, source_target_pairs={{0,8},{8,16},{16,24},{1,9},{9,17},{17,25},{2,10},{10,18},{18,26},{... | collective-permute-start | bytes 1277960 | tf_op jit(solution)/shard_map/ppermute | solution.py:32
  13.1 0.8 copy-start.4
  15.1 25.1 %all-to-all-start = ((f32[1,208,512]{1,0,2:T(1,128)}), f32[1,208,512]{1,0,2:T(1,128)S(1)}, u32[]{:S(2)}, u32[]{:S(2)}) async-start(f32[1,208,512]{1,0,2:T(1,128)} %copy.57), calls=%async_computation | async-start | bytes 1048576 | tf_op jit(solution)/shard_map/all_to_all | solution.py:40
  20.9 69.0 %collective-permute-start.6 = (f32[26,4,1,512]{3,0,2,1:T(8,128)}, f32[26,4,1,512]{3,0,2,1:T(8,128)}, u32[]{:S(2)}, u32[]{:S(2)}) collective-permute-start(f32[26,4,1,512]{3,0,2,1:T(8,128)} %get-tuple-element.7), channel_id=1, source_target_pairs={{1,0},{3,2},{5,4},{7,6},{9,8},{11,10},{13,12},{15,14},{17,16},{19,... | collective-permute-start | bytes 638984 | tf_op jit(solution)/shard_map/ppermute | solution.py:24
  22.1 67.7 %collective-permute-start.7 = (f32[26,4,1,512]{3,0,2,1:T(8,128)}, f32[26,4,1,512]{3,0,2,1:T(8,128)}, u32[]{:S(2)}, u32[]{:S(2)}) collective-permute-start(f32[26,4,1,512]{3,0,2,1:T(8,128)} %get-tuple-element.8), channel_id=1, source_target_pairs={{0,1},{2,3},{4,5},{6,7},{8,9},{10,11},{12,13},{14,15},{16,17},{18,... | collective-permute-start | bytes 638984 | tf_op jit(solution)/shard_map/ppermute | solution.py:23
  29.3 57.2 %collective-permute-start.4 = (f32[26,4,8,1]{3,0,2,1:T(8,128)}, f32[26,4,8,1]{3,0,2,1:T(8,128)}, u32[]{:S(2)}, u32[]{:S(2)}) collective-permute-start(f32[26,4,8,1]{3,0,2,1:T(8,128)} %get-tuple-element.5), channel_id=1, source_target_pairs={{0,2},{2,4},{4,6},{6,0},{1,3},{3,5},{5,7},{7,1},{8,10},{10,12},{12... | collective-permute-start | bytes 9992 | tf_op jit(solution)/shard_map/ppermute | solution.py:23
  40.3 5.6 %copy-start.9 = (f32[6]{0:T(128)S(1)}, f32[6]{0:T(128)}, u32[]{:S(2)}) copy-start(f32[6]{0:T(128)} %param.17) | copy-start | bytes 76
  40.3 5.6 %copy-start.10 = (f32[6]{0:T(128)S(1)}, f32[6]{0:T(128)}, u32[]{:S(2)}) copy-start(f32[6]{0:T(128)} %param.16) | copy-start | bytes 76
  41.5 17.2 %all-to-all-start.1 = ((f32[4,1,208,128]{3,2,1,0:T(8,128)}), f32[4,1,208,128]{3,2,1,0:T(8,128)S(1)}, u32[]{:S(2)}, u32[]{:S(2)}) async-start(f32[4,1,208,128]{3,2,1,0:T(8,128)} %pad_maximum_fusion.5), calls=%async_computation.1 | async-start | bytes 851968 | tf_op jit(solution)/shard_map/all_to_all | solution.py:44
  58.7 1.3 %copy-start.3 = (f32[20,32,512]{2,1,0:T(8,128)S(1)}, f32[20,32,512]{2,1,0:T(8,128)}, u32[]{:S(2)}) copy-start(f32[20,32,512]{2,1,0:T(8,128)} %slice_bitcast_fusion.1) | copy-start | bytes 3932164
  58.7 1.5 %copy-start.8 = (f32[20,20]{1,0:T(8,128)S(1)}, f32[20,20]{1,0:T(8,128)}, u32[]{:S(2)}) copy-start(f32[20,20]{1,0:T(8,128)} %param.15) | copy-start | bytes 4804
  59.0 14.5 %collective-permute-start.1 = (f32[208,512]{1,0:T(8,128)S(1)}, f32[208,512]{1,0:T(8,128)S(1)}, u32[]{:S(2)}, u32[]{:S(2)}) collective-permute-start(f32[208,512]{1,0:T(8,128)S(1)} %bitcast.66), channel_id=1, source_target_pairs={{6,0},{0,2},{2,4},{4,6},{7,1},{1,3},{3,5},{5,7},{14,8},{8,10},{10,... | collective-permute-start | bytes 1277960 | tf_op jit(solution)/shard_map/ppermute | solution.py:13
  60.2 17.5 %copy-start.11 = (s32[4]{0:T(128)S(1)}, s32[4]{0:T(128)}, u32[]{:S(2)}) copy-start(s32[4]{0:T(128)} %param.20) | copy-start | bytes 52
  73.8 6.6 %collective-permute-start.2 = (f32[208,128]{1,0:T(8,128)S(1)}, f32[208,128]{1,0:T(8,128)S(1)}, u32[]{:S(2)}, u32[]{:S(2)}) collective-permute-start(f32[208,128]{1,0:T(8,128)S(1)} %get-tuple-element.11), channel_id=1, source_target_pairs={{0,2},{2,4},{4,6},{6,0},{1,3},{3,5},{5,7},{7,1},{8,10},{10,12},{12... | collective-permute-start | bytes 319496 | tf_op jit(solution)/shard_map/ppermute | solution.py:23
  73.9 6.5 %collective-permute-start.3 = (f32[208,128]{1,0:T(8,128)S(1)}, f32[208,128]{1,0:T(8,128)S(1)}, u32[]{:S(2)}, u32[]{:S(2)}) collective-permute-start(f32[208,128]{1,0:T(8,128)S(1)} %get-tuple-element.12), channel_id=1, source_target_pairs={{2,0},{4,2},{6,4},{0,6},{3,1},{5,3},{7,5},{1,7},{10,8},{12,10},{14... | collective-permute-start | bytes 319496 | tf_op jit(solution)/shard_map/ppermute | solution.py:24
  80.4 9.5 %collective-permute-start.5 = (f32[26,4,8,1]{3,0,2,1:T(8,128)}, f32[26,4,8,1]{3,0,2,1:T(8,128)}, u32[]{:S(2)}, u32[]{:S(2)}) collective-permute-start(f32[26,4,8,1]{3,0,2,1:T(8,128)} %get-tuple-element.6), channel_id=1, source_target_pairs={{2,0},{4,2},{6,4},{0,6},{3,1},{5,3},{7,5},{1,7},{10,8},{12,10},{14... | collective-permute-start | bytes 9992 | tf_op jit(solution)/shard_map/ppermute | solution.py:24
  81.1 8.8 %slice-start = ((f32[26,4,8,512]{3,0,2,1:T(8,128)}), f32[26,3,8,512]{3,0,2,1:T(8,128)S(1)}, s32[]{:S(2)}) async-start(f32[26,4,8,512]{3,0,2,1:T(8,128)} %copy-done.1), calls=%async_computation.2 | async-start | bytes 3145728 | tf_op jit(solution)/shard_map/slice | solution.py:104
  81.1 8.8 %copy-start.2 = (f32[20,4,8,512]{3,0,2,1:T(8,128)S(1)}, f32[20,4,8,512]{3,0,2,1:T(8,128)}, u32[]{:S(2)}) copy-start(f32[20,4,8,512]{3,0,2,1:T(8,128)} %fusion.9) | copy-start | bytes 3932164
  81.1 8.8 %copy-start.6 = (f32[4,8,512]{2,1,0:T(8,128)S(1)}, f32[4,8,512]{2,1,0:T(8,128)}, u32[]{:S(2)}) copy-start(f32[4,8,512]{2,1,0:T(8,128)} %param.14) | copy-start | bytes 196612
  81.1 8.8 %copy-start.7 = (f32[4,8,512]{2,1,0:T(8,128)S(1)}, f32[4,8,512]{2,1,0:T(8,128)}, u32[]{:S(2)}) copy-start(f32[4,8,512]{2,1,0:T(8,128)} %param.13) | copy-start | bytes 196612
  84.6 5.3 %copy-start.5 = (f32[6,4,8,512]{3,0,2,1:T(8,128)S(1)}, f32[6,4,8,512]{3,0,2,1:T(8,128)}, u32[]{:S(2)}) copy-start(f32[6,4,8,512]{3,0,2,1:T(8,128)} %fusion.11) | copy-start | bytes 1179652
